TPU v7x, 32 devices: a whole 2x2x4 slice. The times are simulated.
32 devices in a mesh: groups: 2 (over y), tm: 4 (over z), section: 4 (over x, core).
Axes of the slice: x: 2, y: 2, z: 4, core: 2. Of those that a mesh axis runs over, the one named last changes fastest.
Arguments:
- states: float32 [16, 1, 4096], P(('groups', 'tm')), parts along dimension 0, may hold values from -6 to 6
- timesteps: int32 [16], P(('groups', 'tm')), parts along dimension 0, may hold values from 0 to 999
- step_sizes: float32 [16], P(('groups', 'tm')), parts along dimension 0, may hold values from 0.05 to 0.2
- labels: int32 [2], P('groups'), parts along dimension 0, may hold values from 0 to 1000
- class_table: bfloat16 [1001, 1152], replicated, may hold values from -6 to 6
- embed_weight: bfloat16 [16, 1152], replicated, may hold values from -1.5 to 1.5
- ada_weight: bfloat16 [4, 1152, 2304], P('section', 'tm'), may hold values from -0.1875 to 0.1875
- up_weight: bfloat16 [4, 1152, 2304], P('section', 'tm'), may hold values from -0.1875 to 0.1875
- down_weight: bfloat16 [4, 2304, 1152], P('section', 'tm'), may hold values from -0.125 to 0.125
- final_weight: bfloat16 [1152, 16], replicated, may hold values from -0.1875 to 0.1875
Outputs:
- new_states: float32 [16, 1, 4096], P(('groups', 'tm'), None, 'section'), parts along dimension 0
- step_err: float32 [16], P(('groups', 'tm')), parts along dimension 0
There are 2 independent parts, one for each index of `groups`. A program takes and returns all parts, laid end to end along the dimension named above; an argument that names none is the same for every part. Nothing has to cross between parts.
All inputs are finite; a program needn't handle non-finite values.
Results may differ from a plain program's by a relative error of at most 0.0065.
Values may be sent and summed in bfloat16 or wider, within the bound.
No kernel may reach another device: no remote copies, remote signals or barrier semaphores. Data moves between devices by JAX's collectives and lax.ppermute only.
A program may use at most 128 MiB of HBM per device.

v0:
```python
import math
import jax
import jax.numpy as jnp
from jax import lax
from jax.sharding import PartitionSpec as P

D = 1152
PATCHES = 256
PCH = 16
P_SIZE = 4096


def passed_along(array, axis, by):
    devices = lax.axis_size(axis)
    pairs = [(i, i + by) for i in range(devices) if 0 <= i + by < devices]
    return lax.ppermute(array, axis, pairs)


def spread_2(block, axis, source):
    block = jnp.where(lax.axis_index(axis) == source, block, jnp.zeros_like(block))
    return lax.psum(block, axis)


def carried_in(part, axis, combine, identity):
    place = lax.axis_index(axis)
    gathered = lax.all_gather(part, axis)
    state = jnp.zeros_like(part) + jnp.asarray(identity, part.dtype)

    def one(lap, state):
        return combine(state, lax.dynamic_index_in_dim(gathered, lap, 0, False))

    return lax.fori_loop(0, place, one, state)


def condition_rows(timesteps, labels, class_table):
    half_width = D // 2
    frequency = jnp.exp(-math.log(10000.0) * jnp.arange(half_width, dtype=jnp.float32) / half_width)
    phases = timesteps.astype(jnp.float32)[:, None] * frequency[None, :]
    timing = jnp.concatenate([jnp.cos(phases), jnp.sin(phases)], axis=1)
    classes = class_table[labels].astype(jnp.float32)
    return jax.nn.silu(timing[:, None, :] + classes[None, :, :]).astype(jnp.bfloat16)


def normalize(values):
    center = values - jnp.mean(values, axis=-1, keepdims=True)
    spread = jnp.mean(center * center, axis=-1, keepdims=True)
    return center * lax.rsqrt(spread + 1e-06)


def apply_layer(hidden, scale_mod, gate_mod, up_proj, down_proj):
    normed = (normalize(hidden) * (1.0 + scale_mod[:, None, :])).astype(jnp.bfloat16)
    inner = jax.nn.gelu(
        jnp.dot(normed.reshape(-1, D), up_proj, preferred_element_type=jnp.float32),
        approximate=True,
    ).astype(jnp.bfloat16)
    branch = jnp.dot(inner, down_proj, preferred_element_type=jnp.float32).reshape(hidden.shape)
    return (hidden + gate_mod[:, None, :] * branch).astype(jnp.bfloat16)


def shards(
    states,
    timesteps,
    step_sizes,
    labels,
    class_table,
    embed_weight,
    ada_weight,
    up_weight,
    down_weight,
    final_weight,
):
    steps_here = states.shape[0]
    batch_here = states.shape[1]
    row_total = steps_here * batch_here
    section_idx = lax.axis_index("section")
    section_count = lax.axis_size("section")
    time_idx = lax.axis_index("tm")
    cond_rows = condition_rows(timesteps, labels, class_table).reshape(row_total, D)
    up_full, down_full = (
        lax.all_gather(up_weight, "tm", axis=1, tiled=True),
        lax.all_gather(down_weight, "tm", axis=1, tiled=True),
    )
    window_cond = lax.all_gather(cond_rows, "tm", axis=0, tiled=True)
    shard_width = ada_weight.shape[1]
    first_col = time_idx * shard_width
    picked = lax.dynamic_slice(
        window_cond, (0, first_col), (row_total * lax.axis_size("tm"), shard_width)
    )
    modulation = lax.psum_scatter(
        jnp.dot(picked, ada_weight[0], preferred_element_type=jnp.float32),
        "tm",
        scatter_dimension=0,
        tiled=True,
    )
    up_proj = up_full[0]
    down_proj = down_full[0]
    scale_mod = modulation[:, :D]
    gate_mod = modulation[:, D:]
    blocks = 1
    per_block = row_total // blocks
    patches = states.reshape(row_total, PATCHES, PCH).astype(jnp.bfloat16)
    is_last = section_idx == section_count - 1

    def tick_step(tick, carry):
        received, drift_rows = carry
        micro_idx = tick - section_idx
        active = (micro_idx >= 0) & (micro_idx < blocks)

        def compute(unused):
            embedded = jnp.dot(
                patches.reshape(-1, PCH), embed_weight, preferred_element_type=jnp.float32
            ).reshape(per_block, PATCHES, D)
            entering = jnp.where(section_idx == 0, embedded, received.astype(jnp.float32))
            return apply_layer(entering, scale_mod, gate_mod, up_proj, down_proj)

        def resting(unused):
            return jnp.zeros((per_block, PATCHES, D), jnp.bfloat16)

        leaving = lax.cond(active, compute, resting, 0)
        normed = normalize(leaving.astype(jnp.float32)).astype(jnp.bfloat16)
        block_drift = jnp.dot(
            normed.reshape(-1, D), final_weight, preferred_element_type=jnp.float32
        ).reshape(per_block, PATCHES, PCH)
        drift_rows = jnp.where(is_last & active, block_drift, drift_rows)
        received = passed_along(leaving, "section", 1)
        return (received, drift_rows)

    start_carry = (
        jnp.zeros((per_block, PATCHES, D), jnp.bfloat16),
        jnp.zeros((row_total, PATCHES, PCH), jnp.float32),
    )
    unused_recv, drift_rows = lax.fori_loop(0, blocks + section_count - 1, tick_step, start_carry)
    drift_rows = spread_2(
        drift_rows.reshape(steps_here, batch_here, P_SIZE), "section", section_count - 1
    )
    shard_cols = P_SIZE // section_count
    col_start = section_idx * shard_cols
    own_drift = lax.dynamic_slice_in_dim(drift_rows, col_start, shard_cols, 2)
    own_states = lax.dynamic_slice_in_dim(states, col_start, shard_cols, 2)
    term_rows = step_sizes[:, None, None] * own_drift
    running = jnp.cumsum(term_rows, axis=0)
    earlier = jnp.concatenate(
        [jnp.zeros((1, batch_here, shard_cols), jnp.float32), running[:-1]], axis=0
    )
    block_total = running[-1]

    def adding(before, after):
        return before + after

    offset_sum = carried_in(block_total, "tm", adding, jnp.zeros_like(block_total))
    first_state = spread_2(own_states[0], "tm", 0)
    new_states = first_state[None] + offset_sum[None] + earlier
    local_err = jnp.max(jnp.abs(new_states - own_states), axis=(1, 2))
    step_err = lax.pmax(local_err, "section")
    return (new_states, step_err)


def solution(mesh):
    return jax.shard_map(
        shards,
        mesh=mesh,
        in_specs=(
            P(("groups", "tm"), None, None),
            P(("groups", "tm")),
            P(("groups", "tm")),
            P("groups"),
            P(),
            P(),
            P("section", "tm", None),
            P("section", "tm", None),
            P("section", "tm", None),
            P(),
        ),
        out_specs=(P(("groups", "tm"), None, "section"), P(("groups", "tm"))),
        check_vma=False,
    )
```

profile of v0, /device:TPU:0, one launch (start us, length us, event | category | flops | bytes accessed | tf_op | source)
XLA Modules:
  0.0 417.9 jit_solution(5465141717596316818)
XLA Ops:
  9.7 14.9 %all-gather = bf16[4,2,1152]{2,1,0:T(2,128)(2,1)S(1)} all-gather(bf16[1,2,1152]{2,1,0:T(2,128)(2,1)S(1)} %fusion.28), channel_id=1, replica_groups=mesh['groups'=2,'tm'=4,'section'=4] {'tm'}, dimensions={0}, use_global_device_ids=true | all-gather | bytes 23040 | tf_op jit(solution)/shard_map/all_gather | solution.py:83
  28.8 11.8 %psum.14 = f32[1,1024]{1,0:T(1,128)S(1)} all-reduce(f32[1,1024]{1,0:T(1,128)S(1)} %fusion.29), channel_id=1, replica_groups=mesh['groups'=2,'tm'=4,'section'=4] {'tm'}, use_global_device_ids=true, to_apply=%region_0.1 | all-reduce | flops 1024 | bytes 8192 | tf_op jit(solution)/shard_map/psum | solution.py:21
  40.5 20.5 %all-reduce.4.cloned.1.call-done = f32[8,2304]{1,0:T(8,128)} async-done(((f32[8,2304]{1,0:T(8,128)}), f32[8,2304]{1,0:T(8,128)}) %all-reduce.4.cloned.1.call-update) | async-done | bytes 73744
  61.9 99.9 %all-gather.6.cloned.1.call-done = bf16[1,2304,1152]{2,1,0:T(8,128)(2,1)} async-done(((bf16[1,576,1152]{2,1,0:T(8,128)(2,1)}), bf16[1,2304,1152]{2,1,0:T(8,128)(2,1)}) %all-gather.6.cloned.1.call-update) | async-done | bytes 5308432 | tf_op jit(solution)/shard_map/all_gather | solution.py:81
  161.8 99.0 %all-gather.4.cloned.1.call-done = bf16[1,1152,2304]{2,1,0:T(8,128)(2,1)} async-done(((bf16[1,288,2304]{2,1,0:T(8,128)(2,1)}), bf16[1,1152,2304]{2,1,0:T(8,128)(2,1)}) %all-gather.4.cloned.1.call-update) | async-done | bytes 5308432 | tf_op jit(solution)/shard_map/all_gather | solution.py:80
  261.0 108.0 %while.28 = (s32[]{:T(128)}, bf16[2,256,1152]{2,1,0:T(8,128)(2,1)S(1)}, f32[2,256,16]{1,2,0:T(8,128)S(1)}, s32[]{:T(128)}, bf16[2,256,16]{1,2,0:T(8,128)(2,1)S(1...) while((s32[]{:T(128)}, ...), condition=%wide.region_9.10_spmd.clone, body=%wide.region_2.9_spmd.clone.sunk | while | flops 5496589824 | bytes 52134240 | solution.py:132
  261.0 20.5 %conditional.3 = (bf16[2,256,1152]{2,1,0:T(8,128)(2,1)}, f32[2,256,1152]{2,1,0:T(8,128)}, f32[2,256,1]{1,0,2:T(2,128)S(1)}) conditional(s32[]{:T(128)} %convert_element_type.90, () %tuple.79, (s32[]{:T(128)}, bf16[2,256,16]{1,2,0:T(8,128)(2,1)S(1)}, bf16[16,1152]{1,0:T(8,128)(2,1)S(1)}, bf16[2,256,1152]{2,1,0:T(8,128)(2,1)S(1)}, ...), branch_computations={%region_3.3_spmd, %region_4.7_spmd} | conditional | flops 5474159104 | bytes 42577984 | solution.py:119
  263.1 11.9 %fusion.8 = f32[512,1152]{1,0:T(8,128)} fusion(bf16[2304,1152]{1,0:T(8,128)(2,1)} %get-tuple-element.231, bf16[512,1152]{1,0:T(8,128)(2,1)S(1)} %bitcast.40, bf16[1152,2304]{1,0:T(8,128)(2,1)} %get-tuple-element.230), kind=kOutput, calls=%fused_computation.10 | convolution fusion | flops 5446434816 | bytes 14155776 | tf_op jit(solution)/shard_map/while/body/eval_jaxpr/cond/branch_1_fun/dot_general | solution.py:56
  275.0 3.7 fusion.31
  278.7 2.8 convert_element_type.54
  281.5 1.4 collective-permute-start
  282.9 2.0 multiply_reduce_fusion.3
  285.0 2.2 fusion.42
  287.2 2.7 conditional.3
  287.2 1.6 broadcast.140
  288.8 1.1 broadcast.139
  290.0 18.4 %collective-permute-start = (bf16[2,256,1152]{2,1,0:T(8,128)(2,1)}, bf16[2,256,1152]{2,1,0:T(8,128)(2,1)S(1)}, u32[]{:S(2)}, u32[]{:S(2)}) collective-permute-start(bf16[2,256,1152]{2,1,0:T(8,128)(2,1)} %get-tuple-element.491), channel_id=1, source_target_pairs={{0,1},{1,2},{2,3},{4,5},{5,6},{6,7},{8,9},{9,10},{10,11},{12,13},{... | collective-permute-start | bytes 3538952 | tf_op jit(solution)/shard_map/while/body/eval_jaxpr/ppermute | solution.py:16
  308.4 2.0 multiply_reduce_fusion.3
  310.4 2.2 fusion.42
  312.7 2.7 conditional.3
  312.7 1.6 broadcast.140
  315.4 11.0 %collective-permute-start = (bf16[2,256,1152]{2,1,0:T(8,128)(2,1)}, bf16[2,256,1152]{2,1,0:T(8,128)(2,1)S(1)}, u32[]{:S(2)}, u32[]{:S(2)}) collective-permute-start(bf16[2,256,1152]{2,1,0:T(8,128)(2,1)} %get-tuple-element.491), channel_id=1, source_target_pairs={{0,1},{1,2},{2,3},{4,5},{5,6},{6,7},{8,9},{9,10},{10,11},{12,13},{... | collective-permute-start | bytes 3538952 | tf_op jit(solution)/shard_map/while/body/eval_jaxpr/ppermute | solution.py:16
  326.4 2.0 multiply_reduce_fusion.3
  328.5 2.2 fusion.42
  330.8 2.7 conditional.3
  330.8 1.6 broadcast.140
  333.5 31.2 %collective-permute-start = (bf16[2,256,1152]{2,1,0:T(8,128)(2,1)}, bf16[2,256,1152]{2,1,0:T(8,128)(2,1)S(1)}, u32[]{:S(2)}, u32[]{:S(2)}) collective-permute-start(bf16[2,256,1152]{2,1,0:T(8,128)(2,1)} %get-tuple-element.491), channel_id=1, source_target_pairs={{0,1},{1,2},{2,3},{4,5},{5,6},{6,7},{8,9},{9,10},{10,11},{12,13},{... | collective-permute-start | bytes 3538952 | tf_op jit(solution)/shard_map/while/body/eval_jaxpr/ppermute | solution.py:16
  364.7 2.0 multiply_reduce_fusion.3
  366.7 2.2 fusion.42
  369.3 21.7 %psum.15 = f32[2,1,4096]{2,0,1:T(2,128)S(1)} all-reduce(f32[2,1,4096]{2,0,1:T(2,128)S(1)} %select_n.84), channel_id=1, replica_groups=mesh['groups'=2,'tm'=4,'section'=4] {'section'}, use_global_device_ids=true, to_apply=%region_10.11 | all-reduce | flops 8192 | bytes 65536 | tf_op jit(solution)/shard_map/psum | solution.py:21
  391.1 13.2 %all_gather.15 = f32[4,1,1024]{2,1,0:T(1,128)S(1)} all-gather(f32[1,1,1024]{2,1,0:T(1,128)S(1)} %get-tuple-element.385), channel_id=1, replica_groups=mesh['groups'=2,'tm'=4,'section'=4] {'tm'}, dimensions={0}, use_global_device_ids=true | all-gather | bytes 20480 | tf_op jit(solution)/shard_map/all_gather | solution.py:26
  405.1 6.3 %pmax.7 = f32[2]{0:T(128)} all-reduce(f32[2]{0:T(128)S(1)} %get-tuple-element.383), channel_id=1, replica_groups=mesh['groups'=2,'tm'=4,'section'=4] {'section'}, use_global_device_ids=true, to_apply=%region_15.16 | all-reduce | flops 2 | bytes 16 | tf_op jit(solution)/shard_map/pmax | solution.py:154
  (71 shorter events, 11.6 us)
Async XLA Ops:
  7.2 17.4 %copy-start = (bf16[1,288,2304]{2,1,0:T(8,128)(2,1)S(1)}, bf16[1,288,2304]{2,1,0:T(8,128)(2,1)}, u32[]{:S(2)}) copy-start(bf16[1,288,2304]{2,1,0:T(8,128)(2,1)} %param.22) | copy-start | bytes 3981316
  7.2 20.3 %copy-start.6 = (u32[32]{0:T(128)S(1)}, u32[32]{0:T(128)}, u32[]{:S(2)}) copy-start(u32[32]{0:T(128)} %constant.144) | copy-start | bytes 388
  7.2 20.0 %copy-start.4 = (f32[2,1,4096]{2,1,0:T(1,128)S(1)}, f32[2,1,4096]{2,1,0:T(1,128)}, u32[]{:S(2)}) copy-start(f32[2,1,4096]{2,1,0:T(1,128)} %param.16) | copy-start | bytes 98308
  7.2 53.9 %all-reduce.4.cloned.1.call-start = ((), (), s32[]{:S(2)}) async-start(), calls=%async_computation.2 | async-start | bytes 147456
  25.6 235.3 %copy-start.2 = (bf16[1152,16]{0,1:T(8,128)(2,1)S(1)}, bf16[1152,16]{0,1:T(8,128)(2,1)}, u32[]{:S(2)}) copy-start(bf16[1152,16]{0,1:T(8,128)(2,1)} %param.25) | copy-start | bytes 110596
  25.6 235.4 %copy-start.3 = (bf16[16,1152]{1,0:T(8,128)(2,1)S(1)}, bf16[16,1152]{1,0:T(8,128)(2,1)}, u32[]{:S(2)}) copy-start(bf16[16,1152]{1,0:T(8,128)(2,1)} %param.21) | copy-start | bytes 110596
  25.6 136.2 %all-gather.6.cloned.1.call-start = ((), (), s32[]{:S(2)}) async-start(), calls=%async_computation.1 | async-start | bytes 6635520 | tf_op jit(solution)/shard_map/all_gather | solution.py:81
  26.4 234.5 %all-gather.4.cloned.1.call-start = ((), (), s32[]{:S(2)}) async-start(), calls=%async_computation | async-start | bytes 6635520 | tf_op jit(solution)/shard_map/all_gather | solution.py:80
  261.0 130.0 %copy-start.5 = (f32[2]{0:T(128)S(1)}, f32[2]{0:T(128)}, u32[]{:S(2)}) copy-start(f32[2]{0:T(128)} %param.18) | copy-start | bytes 28
  261.6 1.4 copy-start.1
  281.5 5.7 %collective-permute-start = (bf16[2,256,1152]{2,1,0:T(8,128)(2,1)}, bf16[2,256,1152]{2,1,0:T(8,128)(2,1)S(1)}, u32[]{:S(2)}, u32[]{:S(2)}) collective-permute-start(bf16[2,256,1152]{2,1,0:T(8,128)(2,1)} %get-tuple-element.491), channel_id=1, source_target_pairs={{0,1},{1,2},{2,3},{4,5},{5,6},{6,7},{8,9},{9,10},{10,11},{12,13},{... | collective-permute-start | bytes 3538952 | tf_op jit(solution)/shard_map/while/body/eval_jaxpr/ppermute | solution.py:16
  290.0 22.7 %collective-permute-start = (bf16[2,256,1152]{2,1,0:T(8,128)(2,1)}, bf16[2,256,1152]{2,1,0:T(8,128)(2,1)S(1)}, u32[]{:S(2)}, u32[]{:S(2)}) collective-permute-start(bf16[2,256,1152]{2,1,0:T(8,128)(2,1)} %get-tuple-element.491), channel_id=1, source_target_pairs={{0,1},{1,2},{2,3},{4,5},{5,6},{6,7},{8,9},{9,10},{10,11},{12,13},{... | collective-permute-start | bytes 3538952 | tf_op jit(solution)/shard_map/while/body/eval_jaxpr/ppermute | solution.py:16
  315.4 15.3 %collective-permute-start = (bf16[2,256,1152]{2,1,0:T(8,128)(2,1)}, bf16[2,256,1152]{2,1,0:T(8,128)(2,1)S(1)}, u32[]{:S(2)}, u32[]{:S(2)}) collective-permute-start(bf16[2,256,1152]{2,1,0:T(8,128)(2,1)} %get-tuple-element.491), channel_id=1, source_target_pairs={{0,1},{1,2},{2,3},{4,5},{5,6},{6,7},{8,9},{9,10},{10,11},{12,13},{... | collective-permute-start | bytes 3538952 | tf_op jit(solution)/shard_map/while/body/eval_jaxpr/ppermute | solution.py:16
  333.5 35.5 %collective-permute-start = (bf16[2,256,1152]{2,1,0:T(8,128)(2,1)}, bf16[2,256,1152]{2,1,0:T(8,128)(2,1)S(1)}, u32[]{:S(2)}, u32[]{:S(2)}) collective-permute-start(bf16[2,256,1152]{2,1,0:T(8,128)(2,1)} %get-tuple-element.491), channel_id=1, source_target_pairs={{0,1},{1,2},{2,3},{4,5},{5,6},{6,7},{8,9},{9,10},{10,11},{12,13},{... | collective-permute-start | bytes 3538952 | tf_op jit(solution)/shard_map/while/body/eval_jaxpr/ppermute | solution.py:16
Sparse Core Ops, SparseCore 0:
  25.8 35.2 all-reduce.3
  62.6 99.1 all-gather.5
  163.4 97.4 all-gather.3
where the time goes:
time: 419 us; the launch traced here: 418 us
  waiting for transfers between devices  221 us (53%)
  blocking collectives  67.9 us (16%)
  starting transfers between devices  62 us (15%)
  matrix products  22.4 us (5%)
  other arithmetic  17.5 us (4%)
  between operations  15.3 us (4%)
  local copies, waits for them, and re-layouts  11.5 us (3%)
    all_gather x1, waiting for transfers between devices, shards(): lax.all_gather(down_weight, 'tm', axis=1, tiled=True)  99.9 us
    all_gather x1, waiting for transfers between devices, shards(): lax.all_gather(up_weight, 'tm', axis=1, tiled=True)  99 us
    ppermute x4, starting transfers between devices, passed_along(): return lax.ppermute(array, axis, pairs)  61.9 us
    psum x2, blocking collectives, spread_2(): return lax.psum(block, axis)  33.5 us
    unnamed x4, waiting for transfers between devices  21.9 us
    all_gather x1, blocking collectives, shards(): window_cond = lax.all_gather(cond_rows, 'tm', axis=0, tiled=True)  14.9 us
    all_gather x1, blocking collectives, carried_in(): gathered = lax.all_gather(part, axis)  13.2 us
    dot_general x1, matrix products, apply_layer(): jnp.dot(inner, down_proj, preferred_element_type=jnp.float32)  11.9 us
  transfers between devices with their start and end apart: 7, of which 3 were waited for; matrix products, arithmetic and copies ran while one was open for 5% of the time, Pallas kernels for 0%

commit v1 on v0

--- a/solution.py
+++ b/solution.py
@@ -78,7 +78,7 @@
     cond_rows = condition_rows(timesteps, labels, class_table).reshape(row_total, D)
     up_full, down_full = (
         lax.all_gather(up_weight, "tm", axis=1, tiled=True),
-        lax.all_gather(down_weight, "tm", axis=1, tiled=True),
+        jnp.concatenate(lax.all_gather(down_weight, "tm"), axis=1),
     )
     window_cond = lax.all_gather(cond_rows, "tm", axis=0, tiled=True)
     shard_width = ada_weight.shape[1]

time: 419 us -> 419 us (level)
  no operation moved by 1% of the time
where the time goes in v1:
time: 419 us; the launch traced here: 418 us
  waiting for transfers between devices  221 us (53%)
  blocking collectives  67.9 us (16%)
  starting transfers between devices  62 us (15%)
  matrix products  22.4 us (5%)
  other arithmetic  17.5 us (4%)
  between operations  15.3 us (4%)
  local copies, waits for them, and re-layouts  11.5 us (3%)
    all_gather x1, waiting for transfers between devices, shards(): lax.all_gather(down_weight, 'tm')  99.9 us
    all_gather x1, waiting for transfers between devices, shards(): lax.all_gather(up_weight, 'tm', axis=1, tiled=True)  99 us
    ppermute x4, starting transfers between devices, passed_along(): return lax.ppermute(array, axis, pairs)  61.9 us
    psum x2, blocking collectives, spread_2(): return lax.psum(block, axis)  33.5 us
    unnamed x4, waiting for transfers between devices  21.9 us
    all_gather x1, blocking collectives, shards(): window_cond = lax.all_gather(cond_rows, 'tm', axis=0, tiled=True)  14.9 us
    all_gather x1, blocking collectives, carried_in(): gathered = lax.all_gather(part, axis)  13.2 us
    dot_general x1, matrix products, apply_layer(): jnp.dot(inner, down_proj, preferred_element_type=jnp.float32)  11.9 us
  transfers between devices with their start and end apart: 7, of which 3 were waited for; matrix products, arithmetic and copies ran while one was open for 5% of the time, Pallas kernels for 0%

profile of v1, /device:TPU:0, one launch (start us, length us, event | category | flops | bytes accessed | tf_op | source)
XLA Modules:
  0.0 417.9 jit_solution(5465141717596316818)
XLA Ops:
  9.7 14.9 %all-gather.1 = bf16[4,2,1152]{2,1,0:T(2,128)(2,1)S(1)} all-gather(bf16[1,2,1152]{2,1,0:T(2,128)(2,1)S(1)} %fusion.28), channel_id=1, replica_groups=mesh['groups'=2,'tm'=4,'section'=4] {'tm'}, dimensions={0}, use_global_device_ids=true | all-gather | bytes 23040 | tf_op jit(solution)/shard_map/all_gather | solution.py:83
  28.8 11.8 %psum.14 = f32[1,1024]{1,0:T(1,128)S(1)} all-reduce(f32[1,1024]{1,0:T(1,128)S(1)} %fusion.29), channel_id=1, replica_groups=mesh['groups'=2,'tm'=4,'section'=4] {'tm'}, use_global_device_ids=true, to_apply=%region_0.1 | all-reduce | flops 1024 | bytes 8192 | tf_op jit(solution)/shard_map/psum | solution.py:21
  40.5 20.5 %all-reduce.4.cloned.1.call-done = f32[8,2304]{1,0:T(8,128)} async-done(((f32[8,2304]{1,0:T(8,128)}), f32[8,2304]{1,0:T(8,128)}) %all-reduce.4.cloned.1.call-update) | async-done | bytes 73744
  61.9 99.9 %all-gather.7.cloned.1.call-done = bf16[4,576,1152]{2,1,0:T(8,128)(2,1)} async-done(((bf16[1,576,1152]{2,1,0:T(8,128)(2,1)}), bf16[4,576,1152]{2,1,0:T(8,128)(2,1)}) %all-gather.7.cloned.1.call-update) | async-done | bytes 5308432 | tf_op jit(solution)/shard_map/all_gather | solution.py:81
  161.8 99.0 %all-gather.5.cloned.1.call-done = bf16[1,1152,2304]{2,1,0:T(8,128)(2,1)} async-done(((bf16[1,288,2304]{2,1,0:T(8,128)(2,1)}), bf16[1,1152,2304]{2,1,0:T(8,128)(2,1)}) %all-gather.5.cloned.1.call-update) | async-done | bytes 5308432 | tf_op jit(solution)/shard_map/all_gather | solution.py:80
  261.0 108.0 %while.28 = (s32[]{:T(128)}, bf16[2,256,1152]{2,1,0:T(8,128)(2,1)S(1)}, f32[2,256,16]{1,2,0:T(8,128)S(1)}, s32[]{:T(128)}, bf16[2,256,16]{1,2,0:T(8,128)(2,1)S(1...) while((s32[]{:T(128)}, ...), condition=%wide.region_9.10_spmd.clone, body=%wide.region_2.9_spmd.clone.sunk | while | flops 5496589824 | bytes 52134240 | solution.py:132
  261.0 20.5 %conditional.3 = (bf16[2,256,1152]{2,1,0:T(8,128)(2,1)}, f32[2,256,1152]{2,1,0:T(8,128)}, f32[2,256,1]{1,0,2:T(2,128)S(1)}) conditional(s32[]{:T(128)} %convert_element_type.90, () %tuple.79, (s32[]{:T(128)}, bf16[2,256,16]{1,2,0:T(8,128)(2,1)S(1)}, bf16[16,1152]{1,0:T(8,128)(2,1)S(1)}, bf16[2,256,1152]{2,1,0:T(8,128)(2,1)S(1)}, ...), branch_computations={%region_3.3_spmd, %region_4.7_spmd} | conditional | flops 5474159104 | bytes 42577984 | solution.py:119
  263.1 11.9 %fusion.8 = f32[512,1152]{1,0:T(8,128)} fusion(bf16[2304,1152]{1,0:T(8,128)(2,1)} %get-tuple-element.231, bf16[512,1152]{1,0:T(8,128)(2,1)S(1)} %bitcast.40, bf16[1152,2304]{1,0:T(8,128)(2,1)} %get-tuple-element.230), kind=kOutput, calls=%fused_computation.10 | convolution fusion | flops 5446434816 | bytes 14155776 | tf_op jit(solution)/shard_map/while/body/eval_jaxpr/cond/branch_1_fun/dot_general | solution.py:56
  275.0 3.7 fusion.31
  278.7 2.8 convert_element_type.54
  281.5 1.4 collective-permute-start
  282.9 2.0 multiply_reduce_fusion.3
  285.0 2.2 fusion.42
  287.2 2.7 conditional.3
  287.2 1.6 broadcast.140
  288.8 1.1 broadcast.139
  290.0 18.4 %collective-permute-start = (bf16[2,256,1152]{2,1,0:T(8,128)(2,1)}, bf16[2,256,1152]{2,1,0:T(8,128)(2,1)S(1)}, u32[]{:S(2)}, u32[]{:S(2)}) collective-permute-start(bf16[2,256,1152]{2,1,0:T(8,128)(2,1)} %get-tuple-element.491), channel_id=1, source_target_pairs={{0,1},{1,2},{2,3},{4,5},{5,6},{6,7},{8,9},{9,10},{10,11},{12,13},{... | collective-permute-start | bytes 3538952 | tf_op jit(solution)/shard_map/while/body/eval_jaxpr/ppermute | solution.py:16
  308.4 2.0 multiply_reduce_fusion.3
  310.4 2.2 fusion.42
  312.7 2.7 conditional.3
  312.7 1.6 broadcast.140
  315.4 11.0 %collective-permute-start = (bf16[2,256,1152]{2,1,0:T(8,128)(2,1)}, bf16[2,256,1152]{2,1,0:T(8,128)(2,1)S(1)}, u32[]{:S(2)}, u32[]{:S(2)}) collective-permute-start(bf16[2,256,1152]{2,1,0:T(8,128)(2,1)} %get-tuple-element.491), channel_id=1, source_target_pairs={{0,1},{1,2},{2,3},{4,5},{5,6},{6,7},{8,9},{9,10},{10,11},{12,13},{... | collective-permute-start | bytes 3538952 | tf_op jit(solution)/shard_map/while/body/eval_jaxpr/ppermute | solution.py:16
  326.4 2.0 multiply_reduce_fusion.3
  328.5 2.2 fusion.42
  330.8 2.7 conditional.3
  330.8 1.6 broadcast.140
  333.5 31.2 %collective-permute-start = (bf16[2,256,1152]{2,1,0:T(8,128)(2,1)}, bf16[2,256,1152]{2,1,0:T(8,128)(2,1)S(1)}, u32[]{:S(2)}, u32[]{:S(2)}) collective-permute-start(bf16[2,256,1152]{2,1,0:T(8,128)(2,1)} %get-tuple-element.491), channel_id=1, source_target_pairs={{0,1},{1,2},{2,3},{4,5},{5,6},{6,7},{8,9},{9,10},{10,11},{12,13},{... | collective-permute-start | bytes 3538952 | tf_op jit(solution)/shard_map/while/body/eval_jaxpr/ppermute | solution.py:16
  364.7 2.0 multiply_reduce_fusion.3
  366.7 2.2 fusion.42
  369.3 21.7 %psum.15 = f32[2,1,4096]{2,0,1:T(2,128)S(1)} all-reduce(f32[2,1,4096]{2,0,1:T(2,128)S(1)} %select_n.84), channel_id=1, replica_groups=mesh['groups'=2,'tm'=4,'section'=4] {'section'}, use_global_device_ids=true, to_apply=%region_10.11 | all-reduce | flops 8192 | bytes 65536 | tf_op jit(solution)/shard_map/psum | solution.py:21
  391.1 13.2 %all_gather.19 = f32[4,1,1024]{2,1,0:T(1,128)S(1)} all-gather(f32[1,1,1024]{2,1,0:T(1,128)S(1)} %get-tuple-element.385), channel_id=1, replica_groups=mesh['groups'=2,'tm'=4,'section'=4] {'tm'}, dimensions={0}, use_global_device_ids=true | all-gather | bytes 20480 | tf_op jit(solution)/shard_map/all_gather | solution.py:26
  405.1 6.3 %pmax.7 = f32[2]{0:T(128)} all-reduce(f32[2]{0:T(128)S(1)} %get-tuple-element.383), channel_id=1, replica_groups=mesh['groups'=2,'tm'=4,'section'=4] {'section'}, use_global_device_ids=true, to_apply=%region_15.16 | all-reduce | flops 2 | bytes 16 | tf_op jit(solution)/shard_map/pmax | solution.py:154
  (71 shorter events, 11.6 us)
Async XLA Ops:
  7.2 17.4 %copy-start = (bf16[1,288,2304]{2,1,0:T(8,128)(2,1)S(1)}, bf16[1,288,2304]{2,1,0:T(8,128)(2,1)}, u32[]{:S(2)}) copy-start(bf16[1,288,2304]{2,1,0:T(8,128)(2,1)} %param.22) | copy-start | bytes 3981316
  7.2 20.3 %copy-start.6 = (u32[32]{0:T(128)S(1)}, u32[32]{0:T(128)}, u32[]{:S(2)}) copy-start(u32[32]{0:T(128)} %constant.144) | copy-start | bytes 388
  7.2 20.0 %copy-start.4 = (f32[2,1,4096]{2,1,0:T(1,128)S(1)}, f32[2,1,4096]{2,1,0:T(1,128)}, u32[]{:S(2)}) copy-start(f32[2,1,4096]{2,1,0:T(1,128)} %param.16) | copy-start | bytes 98308
  7.2 53.9 %all-reduce.4.cloned.1.call-start = ((), (), s32[]{:S(2)}) async-start(), calls=%async_computation.2 | async-start | bytes 147456
  25.6 235.3 %copy-start.2 = (bf16[1152,16]{0,1:T(8,128)(2,1)S(1)}, bf16[1152,16]{0,1:T(8,128)(2,1)}, u32[]{:S(2)}) copy-start(bf16[1152,16]{0,1:T(8,128)(2,1)} %param.25) | copy-start | bytes 110596
  25.6 235.4 %copy-start.3 = (bf16[16,1152]{1,0:T(8,128)(2,1)S(1)}, bf16[16,1152]{1,0:T(8,128)(2,1)}, u32[]{:S(2)}) copy-start(bf16[16,1152]{1,0:T(8,128)(2,1)} %param.21) | copy-start | bytes 110596
  25.6 136.2 %all-gather.7.cloned.1.call-start = ((), (), s32[]{:S(2)}) async-start(), calls=%async_computation.1 | async-start | bytes 6635520 | tf_op jit(solution)/shard_map/all_gather | solution.py:81
  26.4 234.5 %all-gather.5.cloned.1.call-start = ((), (), s32[]{:S(2)}) async-start(), calls=%async_computation | async-start | bytes 6635520 | tf_op jit(solution)/shard_map/all_gather | solution.py:80
  261.0 130.0 %copy-start.5 = (f32[2]{0:T(128)S(1)}, f32[2]{0:T(128)}, u32[]{:S(2)}) copy-start(f32[2]{0:T(128)} %param.18) | copy-start | bytes 28
  261.6 1.4 copy-start.1
  281.5 5.7 %collective-permute-start = (bf16[2,256,1152]{2,1,0:T(8,128)(2,1)}, bf16[2,256,1152]{2,1,0:T(8,128)(2,1)S(1)}, u32[]{:S(2)}, u32[]{:S(2)}) collective-permute-start(bf16[2,256,1152]{2,1,0:T(8,128)(2,1)} %get-tuple-element.491), channel_id=1, source_target_pairs={{0,1},{1,2},{2,3},{4,5},{5,6},{6,7},{8,9},{9,10},{10,11},{12,13},{... | collective-permute-start | bytes 3538952 | tf_op jit(solution)/shard_map/while/body/eval_jaxpr/ppermute | solution.py:16
  290.0 22.7 %collective-permute-start = (bf16[2,256,1152]{2,1,0:T(8,128)(2,1)}, bf16[2,256,1152]{2,1,0:T(8,128)(2,1)S(1)}, u32[]{:S(2)}, u32[]{:S(2)}) collective-permute-start(bf16[2,256,1152]{2,1,0:T(8,128)(2,1)} %get-tuple-element.491), channel_id=1, source_target_pairs={{0,1},{1,2},{2,3},{4,5},{5,6},{6,7},{8,9},{9,10},{10,11},{12,13},{... | collective-permute-start | bytes 3538952 | tf_op jit(solution)/shard_map/while/body/eval_jaxpr/ppermute | solution.py:16
  315.4 15.3 %collective-permute-start = (bf16[2,256,1152]{2,1,0:T(8,128)(2,1)}, bf16[2,256,1152]{2,1,0:T(8,128)(2,1)S(1)}, u32[]{:S(2)}, u32[]{:S(2)}) collective-permute-start(bf16[2,256,1152]{2,1,0:T(8,128)(2,1)} %get-tuple-element.491), channel_id=1, source_target_pairs={{0,1},{1,2},{2,3},{4,5},{5,6},{6,7},{8,9},{9,10},{10,11},{12,13},{... | collective-permute-start | bytes 3538952 | tf_op jit(solution)/shard_map/while/body/eval_jaxpr/ppermute | solution.py:16
  333.5 35.5 %collective-permute-start = (bf16[2,256,1152]{2,1,0:T(8,128)(2,1)}, bf16[2,256,1152]{2,1,0:T(8,128)(2,1)S(1)}, u32[]{:S(2)}, u32[]{:S(2)}) collective-permute-start(bf16[2,256,1152]{2,1,0:T(8,128)(2,1)} %get-tuple-element.491), channel_id=1, source_target_pairs={{0,1},{1,2},{2,3},{4,5},{5,6},{6,7},{8,9},{9,10},{10,11},{12,13},{... | collective-permute-start | bytes 3538952 | tf_op jit(solution)/shard_map/while/body/eval_jaxpr/ppermute | solution.py:16
Sparse Core Ops, SparseCore 0:
  25.8 35.2 all-reduce.3
  62.6 99.1 all-gather.6
  163.4 97.4 all-gather.4
